TPU v7x, 32 devices: a whole 2x2x4 slice. The times are simulated.
32 devices in a mesh: groups: 2 (over y), plane: 4 (over z), depth: 2 (over x), tok: 2 (over core).
Axes of the slice: x: 2, y: 2, z: 4, core: 2. Of those that a mesh axis runs over, the one named last changes fastest.
Arguments:
- tokens: bfloat16 [256, 2048], P(('groups', 'plane', 'depth', 'tok')), parts along dimension 0, may hold values from -6 to 6
- expert_ids: int32 [256, 4], P(('groups', 'plane', 'depth', 'tok')), parts along dimension 0, may hold values from 0 to 3, as said below
- slot_index: int32 [256, 4], P(('groups', 'plane', 'depth', 'tok')), parts along dimension 0, may hold values from 0 to 7, as said below
- route_weight: bfloat16 [256, 4], P(('groups', 'plane', 'depth', 'tok')), parts along dimension 0, may hold values from 0.099609375 to 1
- shared_gate: bfloat16 [2048], replicated, may hold values from -0.125 to 0.125
- shared_gate_up: bfloat16 [2, 2048, 5632], P(None, None, 'plane'), may hold values from -0.125 to 0.125
- shared_down: bfloat16 [5632, 2048], P('plane'), may hold values from -0.078125 to 0.078125
- expert_gate_up: bfloat16 [4, 2, 2048, 1408], P('plane', None, None, ('depth', 'tok')), may hold values from -0.125 to 0.125
- expert_down: bfloat16 [4, 1408, 2048], P('plane', ('depth', 'tok')), may hold values from -0.15625 to 0.15625
Outputs:
- mixed: bfloat16 [256, 2048], P(('groups', 'plane', 'depth', 'tok')), parts along dimension 0
There are 2 independent parts, one for each index of `groups`. A program takes and returns all parts, laid end to end along the dimension named above; an argument that names none is the same for every part. Nothing has to cross between parts.
Inputs may be any that keep to these rules, and one draw needn't show every extreme that they name: `expert_ids`: each row names 4 different experts. Among the choices of the rows of one device that name the same expert, slot_index takes each value from 0 to their count minus one exactly once, in an order that varies from draw to draw; the capacity 8 is filled on some devices.
All inputs are finite; a program needn't handle non-finite values.
Results may differ from a plain program's by a relative error of at most 0.019.
Values may be sent and summed in bfloat16 or wider, within the bound.
A program may use at most 64 MiB of HBM per device.

v0:
```python
import jax
import jax.numpy as jnp
from jax import lax
from jax.sharding import PartitionSpec as P


def gated_rows(token_rows, gate_up):
    gate_part = jnp.dot(token_rows, gate_up[0], preferred_element_type=jnp.float32)
    up_part = jnp.dot(token_rows, gate_up[1], preferred_element_type=jnp.float32)
    return (jax.nn.silu(gate_part) * up_part).astype(jnp.bfloat16)


def expert_rows(received, gate_up, down_proj):
    hidden = gated_rows(lax.all_gather(received, ("depth", "tok"), axis=0, tiled=True), gate_up)
    return lax.psum_scatter(
        jnp.dot(hidden, down_proj, preferred_element_type=jnp.float32).astype(jnp.bfloat16),
        ("depth", "tok"),
        scatter_dimension=0,
        tiled=True,
    ).astype(jnp.float32)


def on_device(
    tokens,
    expert_ids,
    slot_index,
    route_weight,
    shared_gate,
    shared_gate_up,
    shared_down,
    expert_gate_up,
    expert_down,
):
    planes = lax.axis_size("plane")
    tok_rows = tokens.shape[0]
    choose_count = expert_ids.shape[1]
    model_width = tokens.shape[1]
    capacity = max(2, tok_rows * choose_count // planes)
    slot_total = planes * capacity
    local_gate_up = expert_gate_up[0]
    local_down = expert_down[0]
    column = lax.broadcasted_iota(jnp.int32, (slot_total, 1, 1), 0)
    kept_mask = slot_index < capacity
    target = jnp.where(kept_mask, expert_ids * capacity + slot_index, -1)
    matches = target[None, :, :] == column
    spread = jnp.any(matches, axis=2).astype(jnp.bfloat16)
    outgoing = jnp.dot(spread, tokens, preferred_element_type=jnp.float32).astype(jnp.bfloat16)
    outgoing = outgoing.reshape(planes, capacity, model_width)
    routed_slots = lax.all_to_all(
        expert_rows(
            lax.all_to_all(outgoing, "plane", split_axis=0, concat_axis=0, tiled=True),
            local_gate_up,
            local_down,
        ).astype(jnp.bfloat16),
        "plane",
        split_axis=0,
        concat_axis=0,
        tiled=True,
    ).astype(jnp.float32)
    weights = route_weight.astype(jnp.float32)
    combine = jnp.sum(jnp.where(matches, weights[None, :, :], 0.0), axis=2).T
    routed = jnp.dot(
        combine,
        routed_slots.reshape(slot_total, model_width),
        precision=lax.Precision.HIGHEST,
        preferred_element_type=jnp.float32,
    )
    shared_hidden = gated_rows(lax.all_gather(tokens, "plane", axis=0, tiled=True), shared_gate_up)
    shared_out = lax.psum_scatter(
        jnp.dot(shared_hidden, shared_down, preferred_element_type=jnp.float32).astype(
            jnp.bfloat16
        ),
        "plane",
        scatter_dimension=0,
        tiled=True,
    ).astype(jnp.float32)
    shared_scale = jax.nn.sigmoid(jnp.dot(tokens, shared_gate, preferred_element_type=jnp.float32))
    result = shared_scale[:, None] * shared_out + routed
    return result.astype(jnp.bfloat16)


def solution(mesh):
    in_specs = (
        P(("groups", "plane", "depth", "tok"), None),
        P(("groups", "plane", "depth", "tok"), None),
        P(("groups", "plane", "depth", "tok"), None),
        P(("groups", "plane", "depth", "tok"), None),
        P(),
        P(None, None, "plane"),
        P("plane", None),
        P("plane", None, None, ("depth", "tok")),
        P("plane", ("depth", "tok"), None),
    )
    out_specs = P(("groups", "plane", "depth", "tok"), None)
    return jax.shard_map(
        on_device, mesh=mesh, in_specs=in_specs, out_specs=out_specs, check_vma=False
    )
```

profile of v0, /device:TPU:0, one launch (start us, length us, event | category | flops | bytes accessed | tf_op | source)
XLA Modules:
  0.0 94.5 jit_solution(18416283824460108339)
XLA Ops:
  6.5 0.0 copy-start
  6.5 0.8 add_select_fusion
  7.4 0.1 fusion.48
  7.4 1.6 %fusion.12 = bf16[4,8,2048]{2,1,0:T(8,128)(2,1)} fusion(pred[32,8]{0,1:T(8,128)(4,1)S(1)} %fusion.48, bf16[8,2048]{1,0:T(8,128)(2,1)} %param.9), kind=kOutput, calls=%fused_computation.11 | convolution fusion | flops 1114112 | bytes 164096 | tf_op jit(solution)/shard_map/dot_general | solution.py:47
  9.1 6.3 %all-to-all-start = ((bf16[4,8,2048]{2,1,0:T(8,128)(2,1)}), bf16[4,8,2048]{2,1,0:T(8,128)(2,1)S(1)}, u32[]{:S(2)}, u32[]{:S(2)}) async-start(bf16[4,8,2048]{2,1,0:T(8,128)(2,1)} %fusion.12), calls=%async_computation.1 | async-start | bytes 262144 | tf_op jit(solution)/shard_map/all_to_all | solution.py:51
  15.4 0.0 reduce-scatter.5.cloned.1.call-start
  15.4 14.1 %all_gather.6 = bf16[32,2048]{1,0:T(8,128)(2,1)S(1)} all-gather(bf16[8,2048]{1,0:T(8,128)(2,1)} %param.9), channel_id=1, replica_groups=mesh['groups'=2,'plane'=4,'depth'=2,'tok'=2] {'plane'}, dimensions={0}, use_global_device_ids=true | all-gather | bytes 163840 | tf_op jit(solution)/shard_map/all_gather | solution.py:68
  29.6 0.0 all-to-all-done
  29.6 7.2 %all_gather.7 = bf16[16,8,2048]{2,1,0:T(8,128)(2,1)S(1)} all-gather(bf16[4,8,2048]{2,1,0:T(8,128)(2,1)S(1)} %all-to-all-done), channel_id=1, replica_groups=mesh['groups'=2,'plane'=4,'depth'=2,'tok'=2] {'depth','tok'}, dimensions={0}, use_global_device_ids=true | all-gather | bytes 655360 | tf_op jit(solution)/shard_map/all_gather | solution.py:14
  36.7 2.0 %fusion.16 = f32[16,8,352]{2,1,0:T(8,128)S(1)} fusion(bf16[16,8,2048]{2,1,0:T(8,128)(2,1)S(1)} %all_gather.7, bf16[1,2,2048,352]{2,3,1,0:T(8,128)(2,1)} %param.16), kind=kOutput, calls=%fused_computation.16 | convolution fusion | flops 184549376 | bytes 2146304 | tf_op jit(solution)/shard_map/dot_general | solution.py:8
  38.7 0.0 copy-done
  38.7 3.4 %convolution_convert_fusion = bf16[16,8,2048]{2,1,0:T(8,128)(2,1)} fusion(bf16[1,352,2048]{2,1,0:T(8,128)(2,1)S(1)} %copy-done, bf16[16,8,2048]{2,1,0:T(8,128)(2,1)S(1)} %all_gather.7, bf16[1,2,2048,352]{2,3,1,0:T(8,128)(2,1)} %param.16, f32[16,8,352]{2,1,0:T(8,128)S(1)} %fusion.16), kind=kOutput, calls=%fused_computation.6 | convolution fusion | flops 369631232 | bytes 4112384 | tf_op jit(solution)/shard_map/dot_general | solution.py:16
  42.1 0.0 reduce-scatter.5.cloned.1.call-update
  42.1 0.0 reduce-scatter.3.cloned.1.call-start
  42.2 3.7 %fusion.2 = f32[32,1408]{1,0:T(8,128)S(1)} fusion(bf16[32,2048]{1,0:T(8,128)(2,1)S(1)} %all_gather.6, bf16[2,2048,1408]{2,1,0:T(8,128)(2,1)} %param.14), kind=kOutput, calls=%fused_computation.2 | convolution fusion | flops 184549376 | bytes 6078464 | tf_op jit(solution)/shard_map/dot_general | solution.py:8
  45.8 0.0 copy-start.3
  45.8 0.0 copy-start.2
  45.9 0.0 copy-start.1
  45.9 7.2 %convolution_convert_fusion.2 = bf16[32,2048]{1,0:T(8,128)(2,1)} fusion(bf16[1408,2048]{1,0:T(8,128)(2,1)} %param.15, bf16[32,2048]{1,0:T(8,128)(2,1)S(1)} %all_gather.6, bf16[2,2048,1408]{2,1,0:T(8,128)(2,1)} %param.14, f32[32,1408]{1,0:T(8,128)S(1)} %fusion.2), kind=kOutput, calls=%fused_computation.10 | convolution fusion | flops 369434624 | bytes 11976704 | tf_op jit(solution)/shard_map/dot_general | solution.py:70
  53.1 0.0 reduce-scatter.3.cloned.1.call-update
  53.1 0.0 copy-done.3
  53.1 0.1 select_reduce_fusion
  53.2 0.0 copy-done.2
  53.2 11.1 %reduce-scatter.5.cloned.1.call-done = bf16[4,8,2048]{2,1,0:T(8,128)(2,1)} async-done(((bf16[16,8,2048]{2,1,0:T(8,128)(2,1)}), bf16[4,8,2048]{2,1,0:T(8,128)(2,1)}) %reduce-scatter.5.cloned.1.call-update) | async-done | bytes 131088 | tf_op jit(solution)/shard_map/reduce_scatter | solution.py:15
  64.3 4.6 %all-to-all-start.1 = ((bf16[4,8,2048]{2,1,0:T(8,128)(2,1)}), bf16[4,8,2048]{2,1,0:T(8,128)(2,1)S(1)}, u32[]{:S(2)}, u32[]{:S(2)}) async-start(bf16[4,8,2048]{2,1,0:T(8,128)(2,1)} %reduce-scatter.5.cloned.1.call-done), calls=%async_computation.3 | async-start | bytes 262144 | tf_op jit(solution)/shard_map/all_to_all | solution.py:49
  68.9 0.0 copy-done.1
  69.0 0.1 fusion.32
  69.1 17.0 %reduce-scatter.3.cloned.1.call-done = bf16[8,2048]{1,0:T(8,128)(2,1)} async-done(((bf16[32,2048]{1,0:T(8,128)(2,1)}), bf16[8,2048]{1,0:T(8,128)(2,1)}) %reduce-scatter.3.cloned.1.call-update) | async-done | bytes 32784 | tf_op jit(solution)/shard_map/reduce_scatter | solution.py:69
  86.1 0.0 all-to-all-done.1
  86.1 1.5 %fusion.13 = bf16[8,2048]{1,0:T(8,128)(2,1)} fusion(f32[32,8]{0,1:T(8,128)S(1)} %select_reduce_fusion, bf16[4,8,2048]{2,1,0:T(8,128)(2,1)S(1)} %all-to-all-done.1, bf16[8,2048]{1,0:T(8,128)(2,1)} %reduce-scatter.3.cloned.1.call-done, f32[8]{0:T(128)S(1)} %fusion.32), kind=kOutput, calls=%fused_computation.13 | convolution fusion | flops 6356992 | bytes 197664 | tf_op jit(solution)/shard_map/dot_general | solution.py:62
  (2 shorter events, 0.0 us)
Async XLA Ops:
  6.5 32.2 %copy-start = (bf16[1,352,2048]{2,1,0:T(8,128)(2,1)S(1)}, bf16[1,352,2048]{2,1,0:T(8,128)(2,1)}, u32[]{:S(2)}) copy-start(bf16[1,352,2048]{2,1,0:T(8,128)(2,1)} %param.17) | copy-start | bytes 4325380
  9.1 20.5 %all-to-all-start = ((bf16[4,8,2048]{2,1,0:T(8,128)(2,1)}), bf16[4,8,2048]{2,1,0:T(8,128)(2,1)S(1)}, u32[]{:S(2)}, u32[]{:S(2)}) async-start(bf16[4,8,2048]{2,1,0:T(8,128)(2,1)} %fusion.12), calls=%async_computation.1 | async-start | bytes 262144 | tf_op jit(solution)/shard_map/all_to_all | solution.py:51
  15.4 48.9 %reduce-scatter.5.cloned.1.call-start = ((), (), s32[]{:S(2)}) async-start(), calls=%async_computation.5 | async-start | bytes 655360 | tf_op jit(solution)/shard_map/reduce_scatter | solution.py:15
  42.1 44.0 %reduce-scatter.3.cloned.1.call-start = ((), (), s32[]{:S(2)}) async-start(), calls=%async_computation.4 | async-start | bytes 163840 | tf_op jit(solution)/shard_map/reduce_scatter | solution.py:69
  45.8 7.3 %copy-start.3 = (bf16[8,4]{0,1:T(4,128)(2,1)S(1)}, bf16[8,4]{0,1:T(4,128)(2,1)}, u32[]{:S(2)}) copy-start(bf16[8,4]{0,1:T(4,128)(2,1)} %param.12) | copy-start | bytes 196
  45.8 7.4 %copy-start.2 = (bf16[2048]{0:T(1024)(128)(2,1)S(1)}, bf16[2048]{0:T(1024)(128)(2,1)}, u32[]{:S(2)}) copy-start(bf16[2048]{0:T(1024)(128)(2,1)} %param.13) | copy-start | bytes 12292
  45.9 23.1 %copy-start.1 = (bf16[8,2048]{1,0:T(8,128)(2,1)S(1)}, bf16[8,2048]{1,0:T(8,128)(2,1)}, u32[]{:S(2)}) copy-start(bf16[8,2048]{1,0:T(8,128)(2,1)} %param.9) | copy-start | bytes 98308
  64.3 21.7 %all-to-all-start.1 = ((bf16[4,8,2048]{2,1,0:T(8,128)(2,1)}), bf16[4,8,2048]{2,1,0:T(8,128)(2,1)S(1)}, u32[]{:S(2)}, u32[]{:S(2)}) async-start(bf16[4,8,2048]{2,1,0:T(8,128)(2,1)} %reduce-scatter.5.cloned.1.call-done), calls=%async_computation.3 | async-start | bytes 262144 | tf_op jit(solution)/shard_map/all_to_all | solution.py:49
Sparse Core Ops, SparseCore 0:
  42.2 22.0 reduce-scatter.4
  66.6 19.4 reduce-scatter.2
where the time goes:
time: 95 us; the launch traced here: 94.5 us
  waiting for transfers between devices  28.1 us (30%)
  blocking collectives  21.3 us (22%)
  matrix products  19.5 us (21%)
  between operations  13.5 us (14%)
  starting transfers between devices  11 us (12%)
  other arithmetic  0.97 us (1%)
    reduce_scatter x1, waiting for transfers between devices, on_device(): lax.psum_scatter(jnp.dot(shared_hidden, shared_down, preferred_element_ty...  17 us
    all_gather x1, blocking collectives, on_device(): lax.all_gather(tokens, 'plane', axis=0, tiled=True)  14.1 us
    reduce_scatter x1, waiting for transfers between devices, expert_rows(): lax.psum_scatter(jnp.dot(hidden, down_proj, preferred_element_type=jnp.fl...  11.1 us
    dot_general x1, matrix products, on_device(): jnp.dot(shared_hidden, shared_down, preferred_element_type=jnp.float32)  7.22 us
    all_gather x1, blocking collectives, expert_rows(): lax.all_gather(received, ('depth', 'tok'), axis=0, tiled=True)  7.16 us
    all_to_all x1, starting transfers between devices, on_device(): lax.all_to_all(outgoing, 'plane', split_axis=0, concat_axis=0, tiled=True)  6.35 us
    dot_general x2, matrix products, gated_rows(): jnp.dot(token_rows, gate_up[0], preferred_element_type=jnp.float32)  5.62 us
    all_to_all x1, starting transfers between devices, on_device(): lax.all_to_all(expert_rows(lax.all_to_all(outgoing, 'plane', split_axis=0...  4.6 us
  transfers between devices with their start and end apart: 4, of which 2 were waited for; matrix products, arithmetic and copies ran while one was open for 12% of the time, Pallas kernels for 0%

commit v1 on v0

--- a/solution.py
+++ b/solution.py
@@ -2,6 +2,28 @@
 import jax.numpy as jnp
 from jax import lax
 from jax.sharding import PartitionSpec as P
+
+
+def in_order(blocks, dim):
+    blocks = jnp.moveaxis(blocks, 0, dim)
+    shape = blocks.shape
+    return blocks.reshape(*shape[:dim], shape[dim] * shape[dim + 1], *shape[dim + 2 :])
+
+
+def gather_around(x, axis, dim):
+    length = lax.axis_size(axis)
+    pairs = [(i, (i + 1) % length) for i in range(length)]
+    back = [(b, a) for a, b in pairs]
+    lower, upper = ([], [])
+    for step in range(length - 1):
+        if step % 2 == 0:
+            lower.append(lax.ppermute(lower[-1] if lower else x, axis, pairs))
+        else:
+            upper.append(lax.ppermute(upper[-1] if upper else x, axis, back))
+    tiles = jnp.stack([*lower[::-1], x, *upper])
+    shift = lax.axis_index(axis) - len(lower)
+    tiles = tiles[(jnp.arange(length) - shift) % length]
+    return in_order(tiles, dim)
 
 
 def gated_rows(token_rows, gate_up):
@@ -65,7 +87,7 @@
         precision=lax.Precision.HIGHEST,
         preferred_element_type=jnp.float32,
     )
-    shared_hidden = gated_rows(lax.all_gather(tokens, "plane", axis=0, tiled=True), shared_gate_up)
+    shared_hidden = gated_rows(gather_around(tokens, "plane", 0), shared_gate_up)
     shared_out = lax.psum_scatter(
         jnp.dot(shared_hidden, shared_down, preferred_element_type=jnp.float32).astype(
             jnp.bfloat16

time: 95 us -> 90.5 us (0.953)
  blocking collectives: 21.3 us -> 7.17 us
  starting transfers between devices: 11 us -> 16.9 us
  waiting for transfers between devices: 28.1 us -> 29.8 us
  other arithmetic: 0.97 us -> 2.33 us
    all_gather x1 -> x0, blocking collectives: 14.1 us -> none  [on_device(): lax.all_gather(tokens, 'plane', axis=0, tiled=True)]
    ppermute x0 -> x3, starting transfers between devices: none -> 7.16 us  [the longest x1 5.08 us: gather_around(): upper.append(lax.ppermute(upper[-1] if upper else x, axis, back))]
    ppermute x0 -> x3, waiting for transfers between devices: none -> 4.19 us  [the longest x2 4.18 us: gather_around(): lower.append(lax.ppermute(lower[-1] if lower else x, axis, pairs))]
    reduce_scatter x1, waiting for transfers between devices: 11.1 us -> 8.54 us  [expert_rows(): lax.psum_scatter(jnp.dot(hidden, down_proj, preferred_element_type=jnp.fl...]
    all_to_all x1, starting transfers between devices: 6.35 us -> 5.09 us  [on_device(): lax.all_to_all(outgoing, 'plane', split_axis=0, concat_axis=0, tiled=True)]
  transfers between devices with their start and end apart: 4 -> 7, of which waited for: 2 -> 3; matrix products, arithmetic and copies ran while one was open for 12% -> 17% of each run, Pallas kernels for 0% -> 0%
where the time goes in v1:
time: 90.5 us; the launch traced here: 89.8 us
  waiting for transfers between devices  29.8 us (33%)
  matrix products  19.6 us (22%)
  starting transfers between devices  16.9 us (19%)
  between operations  13.5 us (15%)
  blocking collectives  7.17 us (8%)
  other arithmetic  2.33 us (3%)
    reduce_scatter x1, waiting for transfers between devices, on_device(): lax.psum_scatter(jnp.dot(shared_hidden, shared_down, preferred_element_ty...  17 us
    reduce_scatter x1, waiting for transfers between devices, expert_rows(): lax.psum_scatter(jnp.dot(hidden, down_proj, preferred_element_type=jnp.fl...  8.54 us
    dot_general x1, matrix products, on_device(): jnp.dot(shared_hidden, shared_down, preferred_element_type=jnp.float32)  7.22 us
    all_gather x1, blocking collectives, expert_rows(): lax.all_gather(received, ('depth', 'tok'), axis=0, tiled=True)  7.17 us
    dot_general x2, matrix products, gated_rows(): jnp.dot(token_rows, gate_up[0], preferred_element_type=jnp.float32)  5.62 us
    all_to_all x1, starting transfers between devices, on_device(): lax.all_to_all(outgoing, 'plane', split_axis=0, concat_axis=0, tiled=True)  5.09 us
    ppermute x1, starting transfers between devices, gather_around(): upper.append(lax.ppermute(upper[-1] if upper else x, axis, back))  5.08 us
    all_to_all x1, starting transfers between devices, on_device(): lax.all_to_all(expert_rows(lax.all_to_all(outgoing, 'plane', split_axis=0...  4.6 us
  transfers between devices with their start and end apart: 7, of which 3 were waited for; matrix products, arithmetic and copies ran while one was open for 17% of the time, Pallas kernels for 0%

profile of v1, /device:TPU:0, one launch (start us, length us, event | category | flops | bytes accessed | tf_op | source)
XLA Modules:
  0.0 89.8 jit_solution(17180111646039427757)
XLA Ops:
  6.5 0.0 copy-start
  6.5 5.1 %collective-permute-start.2 = (bf16[8,2048]{1,0:T(8,128)(2,1)}, bf16[8,2048]{1,0:T(8,128)(2,1)S(1)}, u32[]{:S(2)}, u32[]{:S(2)}) collective-permute-start(bf16[8,2048]{1,0:T(8,128)(2,1)} %param.9), channel_id=1, source_target_pairs={{4,0},{8,4},{12,8},{0,12},{5,1},{9,5},{13,9},{1,13},{6,2},{10,6},{... | collective-permute-start | bytes 98312 | tf_op jit(solution)/shard_map/ppermute | solution.py:22
  11.6 0.0 collective-permute-start
  11.6 0.7 add_select_fusion
  12.3 0.1 fusion.51
  12.4 1.6 %fusion.12 = bf16[4,8,2048]{2,1,0:T(8,128)(2,1)} fusion(pred[32,8]{0,1:T(8,128)(4,1)S(1)} %fusion.51, bf16[8,2048]{1,0:T(8,128)(2,1)} %param.9), kind=kOutput, calls=%fused_computation.12 | convolution fusion | flops 1114112 | bytes 164096 | tf_op jit(solution)/shard_map/dot_general | solution.py:69
  14.0 5.1 %all-to-all-start = ((bf16[4,8,2048]{2,1,0:T(8,128)(2,1)}), bf16[4,8,2048]{2,1,0:T(8,128)(2,1)S(1)}, u32[]{:S(2)}, u32[]{:S(2)}) async-start(bf16[4,8,2048]{2,1,0:T(8,128)(2,1)} %fusion.12), calls=%async_computation.1 | async-start | bytes 262144 | tf_op jit(solution)/shard_map/all_to_all | solution.py:73
  19.1 0.0 reduce-scatter.5.cloned.1.call-start
  19.1 0.0 collective-permute-done
  19.2 2.1 %collective-permute-start.1 = (bf16[8,2048]{1,0:T(8,128)(2,1)S(1)}, bf16[8,2048]{1,0:T(8,128)(2,1)S(1)}, u32[]{:S(2)}, u32[]{:S(2)}) collective-permute-start(bf16[8,2048]{1,0:T(8,128)(2,1)S(1)} %collective-permute-done), channel_id=1, source_target_pairs={{0,4},{4,8},{8,12},{12,0},{1,5},{5,9},{9,13},{13,1},{2,6},{6,10},{... | collective-permute-start | bytes 98312 | tf_op jit(solution)/shard_map/ppermute | solution.py:20
  21.2 0.7 convert_element_type.31
  21.9 0.0 collective-permute-done.2
  21.9 4.2 %collective-permute-done.1 = bf16[8,2048]{1,0:T(8,128)(2,1)S(1)} collective-permute-done((bf16[8,2048]{1,0:T(8,128)(2,1)S(1)}, bf16[8,2048]{1,0:T(8,128)(2,1)S(1)}, u32[]{:S(2)}, u32[]{:S(2)}) %collective-permute-start.1) | collective-permute-done | bytes 32800 | tf_op jit(solution)/shard_map/ppermute | solution.py:20
  26.1 0.8 pad_maximum_fusion
  26.9 0.6 gather_fusion
  27.4 0.0 all-to-all-done
  27.5 7.2 %all_gather.3 = bf16[16,8,2048]{2,1,0:T(8,128)(2,1)S(1)} all-gather(bf16[4,8,2048]{2,1,0:T(8,128)(2,1)S(1)} %all-to-all-done), channel_id=1, replica_groups=mesh['groups'=2,'plane'=4,'depth'=2,'tok'=2] {'depth','tok'}, dimensions={0}, use_global_device_ids=true | all-gather | bytes 655360 | tf_op jit(solution)/shard_map/all_gather | solution.py:36
  34.6 2.0 %fusion.16 = f32[16,8,352]{2,1,0:T(8,128)S(1)} fusion(bf16[16,8,2048]{2,1,0:T(8,128)(2,1)S(1)} %all_gather.3, bf16[1,2,2048,352]{2,3,1,0:T(8,128)(2,1)} %param.16), kind=kOutput, calls=%fused_computation.17 | convolution fusion | flops 184549376 | bytes 2146304 | tf_op jit(solution)/shard_map/dot_general | solution.py:30
  36.6 0.0 copy-done
  36.6 3.4 %convolution_convert_fusion = bf16[16,8,2048]{2,1,0:T(8,128)(2,1)} fusion(bf16[1,352,2048]{2,1,0:T(8,128)(2,1)S(1)} %copy-done, bf16[16,8,2048]{2,1,0:T(8,128)(2,1)S(1)} %all_gather.3, bf16[1,2,2048,352]{2,3,1,0:T(8,128)(2,1)} %param.16, f32[16,8,352]{2,1,0:T(8,128)S(1)} %fusion.16), kind=kOutput, calls=%fused_computation.7 | convolution fusion | flops 369631232 | bytes 4112384 | tf_op jit(solution)/shard_map/dot_general | solution.py:38
  40.0 0.0 reduce-scatter.5.cloned.1.call-update
  40.0 0.0 reduce-scatter.3.cloned.1.call-start
  40.1 3.7 %fusion.2 = f32[32,1408]{1,0:T(8,128)S(1)} fusion(bf16[2,2048,1408]{2,1,0:T(8,128)(2,1)} %param.14, bf16[4,8,2048]{2,1,0:T(8,128)(2,1)S(1)} %gather_fusion), kind=kOutput, calls=%fused_computation.3 | convolution fusion | flops 184549376 | bytes 6078464 | tf_op jit(solution)/shard_map/dot_general | solution.py:30
  43.7 0.0 copy-start.2
  43.8 0.0 copy-start.1
  43.8 7.2 %convolution_convert_fusion.2 = bf16[32,2048]{1,0:T(8,128)(2,1)} fusion(bf16[1408,2048]{1,0:T(8,128)(2,1)} %param.15, bf16[2,2048,1408]{2,1,0:T(8,128)(2,1)} %param.14, f32[32,1408]{1,0:T(8,128)S(1)} %fusion.2, bf16[4,8,2048]{2,1,0:T(8,128)(2,1)S(1)} %gather_fusion), kind=kOutput, calls=%fused_computation.11 | convolution fusion | flops 369434624 | bytes 11976704 | tf_op jit(solution)/shard_map/dot_general | solution.py:92
  51.0 0.0 reduce-scatter.3.cloned.1.call-update
  51.0 0.1 select_reduce_fusion
  51.1 0.0 copy-done.2
  51.1 8.5 %reduce-scatter.5.cloned.1.call-done = bf16[4,8,2048]{2,1,0:T(8,128)(2,1)} async-done(((bf16[16,8,2048]{2,1,0:T(8,128)(2,1)}), bf16[4,8,2048]{2,1,0:T(8,128)(2,1)}) %reduce-scatter.5.cloned.1.call-update) | async-done | bytes 131088 | tf_op jit(solution)/shard_map/reduce_scatter | solution.py:37
  59.7 4.6 %all-to-all-start.1 = ((bf16[4,8,2048]{2,1,0:T(8,128)(2,1)}), bf16[4,8,2048]{2,1,0:T(8,128)(2,1)S(1)}, u32[]{:S(2)}, u32[]{:S(2)}) async-start(bf16[4,8,2048]{2,1,0:T(8,128)(2,1)} %reduce-scatter.5.cloned.1.call-done), calls=%async_computation.3 | async-start | bytes 262144 | tf_op jit(solution)/shard_map/all_to_all | solution.py:71
  64.3 0.0 copy-done.1
  64.3 0.1 fusion.32
  64.4 17.0 %reduce-scatter.3.cloned.1.call-done = bf16[8,2048]{1,0:T(8,128)(2,1)} async-done(((bf16[32,2048]{1,0:T(8,128)(2,1)}), bf16[8,2048]{1,0:T(8,128)(2,1)}) %reduce-scatter.3.cloned.1.call-update) | async-done | bytes 32784 | tf_op jit(solution)/shard_map/reduce_scatter | solution.py:91
  81.4 0.0 all-to-all-done.1
  81.4 1.5 %fusion.13 = bf16[8,2048]{1,0:T(8,128)(2,1)} fusion(f32[32,8]{0,1:T(8,128)S(1)} %select_reduce_fusion, bf16[4,8,2048]{2,1,0:T(8,128)(2,1)S(1)} %all-to-all-done.1, bf16[8,2048]{1,0:T(8,128)(2,1)} %reduce-scatter.3.cloned.1.call-done, f32[8]{0:T(128)S(1)} %fusion.32), kind=kOutput, calls=%fused_computation.14 | convolution fusion | flops 6356992 | bytes 197664 | tf_op jit(solution)/shard_map/dot_general | solution.py:84
  (3 shorter events, 0.0 us)
Async XLA Ops:
  6.5 30.1 %copy-start = (bf16[1,352,2048]{2,1,0:T(8,128)(2,1)S(1)}, bf16[1,352,2048]{2,1,0:T(8,128)(2,1)}, u32[]{:S(2)}) copy-start(bf16[1,352,2048]{2,1,0:T(8,128)(2,1)} %param.17) | copy-start | bytes 4325380
  6.5 15.4 %collective-permute-start.2 = (bf16[8,2048]{1,0:T(8,128)(2,1)}, bf16[8,2048]{1,0:T(8,128)(2,1)S(1)}, u32[]{:S(2)}, u32[]{:S(2)}) collective-permute-start(bf16[8,2048]{1,0:T(8,128)(2,1)} %param.9), channel_id=1, source_target_pairs={{4,0},{8,4},{12,8},{0,12},{5,1},{9,5},{13,9},{1,13},{6,2},{10,6},{... | collective-permute-start | bytes 98312 | tf_op jit(solution)/shard_map/ppermute | solution.py:22
  11.6 7.5 %collective-permute-start = (bf16[8,2048]{1,0:T(8,128)(2,1)}, bf16[8,2048]{1,0:T(8,128)(2,1)S(1)}, u32[]{:S(2)}, u32[]{:S(2)}) collective-permute-start(bf16[8,2048]{1,0:T(8,128)(2,1)} %param.9), channel_id=1, source_target_pairs={{0,4},{4,8},{8,12},{12,0},{1,5},{5,9},{9,13},{13,1},{2,6},{6,10},{... | collective-permute-start | bytes 98312 | tf_op jit(solution)/shard_map/ppermute | solution.py:20
  14.0 13.4 %all-to-all-start = ((bf16[4,8,2048]{2,1,0:T(8,128)(2,1)}), bf16[4,8,2048]{2,1,0:T(8,128)(2,1)S(1)}, u32[]{:S(2)}, u32[]{:S(2)}) async-start(bf16[4,8,2048]{2,1,0:T(8,128)(2,1)} %fusion.12), calls=%async_computation.1 | async-start | bytes 262144 | tf_op jit(solution)/shard_map/all_to_all | solution.py:73
  19.1 40.5 %reduce-scatter.5.cloned.1.call-start = ((), (), s32[]{:S(2)}) async-start(), calls=%async_computation.5 | async-start | bytes 655360 | tf_op jit(solution)/shard_map/reduce_scatter | solution.py:37
  19.2 6.9 %collective-permute-start.1 = (bf16[8,2048]{1,0:T(8,128)(2,1)S(1)}, bf16[8,2048]{1,0:T(8,128)(2,1)S(1)}, u32[]{:S(2)}, u32[]{:S(2)}) collective-permute-start(bf16[8,2048]{1,0:T(8,128)(2,1)S(1)} %collective-permute-done), channel_id=1, source_target_pairs={{0,4},{4,8},{8,12},{12,0},{1,5},{5,9},{9,13},{13,1},{2,6},{6,10},{... | collective-permute-start | bytes 98312 | tf_op jit(solution)/shard_map/ppermute | solution.py:20
  40.0 41.4 %reduce-scatter.3.cloned.1.call-start = ((), (), s32[]{:S(2)}) async-start(), calls=%async_computation.4 | async-start | bytes 163840 | tf_op jit(solution)/shard_map/reduce_scatter | solution.py:91
  43.7 7.4 %copy-start.2 = (bf16[2048]{0:T(1024)(128)(2,1)S(1)}, bf16[2048]{0:T(1024)(128)(2,1)}, u32[]{:S(2)}) copy-start(bf16[2048]{0:T(1024)(128)(2,1)} %param.13) | copy-start | bytes 12292
  43.8 20.5 %copy-start.1 = (bf16[8,2048]{1,0:T(8,128)(2,1)S(1)}, bf16[8,2048]{1,0:T(8,128)(2,1)}, u32[]{:S(2)}) copy-start(bf16[8,2048]{1,0:T(8,128)(2,1)} %param.9) | copy-start | bytes 98308
  59.7 21.8 %all-to-all-start.1 = ((bf16[4,8,2048]{2,1,0:T(8,128)(2,1)}), bf16[4,8,2048]{2,1,0:T(8,128)(2,1)S(1)}, u32[]{:S(2)}, u32[]{:S(2)}) async-start(bf16[4,8,2048]{2,1,0:T(8,128)(2,1)} %reduce-scatter.5.cloned.1.call-done), calls=%async_computation.3 | async-start | bytes 262144 | tf_op jit(solution)/shard_map/all_to_all | solution.py:71
Sparse Core Ops, SparseCore 0:
  40.2 19.4 reduce-scatter.4
  61.9 19.4 reduce-scatter.2
